TPU v7x, 32 devices: a whole 2x2x4 slice. The times are simulated.
32 devices in a mesh: seq: 8 (over y, x, core), dp: 4 (over z).
Axes of the slice: x: 2, y: 2, z: 4, core: 2. Of those that a mesh axis runs over, the one named last changes fastest.
Arguments:
- queries: bfloat16 [8, 512, 4096], P('dp', 'seq'), may hold values from -8 to 8
- unrotated_key_rows: bfloat16 [8, 512, 1024], P('dp', 'seq'), may hold values from -8 to 8
- value_projection_rows: bfloat16 [8, 512, 1024], P('dp', 'seq'), may hold values from -6 to 6
- attention_output_gradient: bfloat16 [8, 512, 4096], P('dp', 'seq'), may hold values from -16 to 16
- normed_hidden_input: bfloat16 [8, 512, 4096], P('dp', 'seq'), may hold values from -6 to 6
- adapter_down_weight: bfloat16 [4096, 64], replicated, may hold values from -0.01171875 to 0.01171875
- adapter_up_weight: bfloat16 [64, 4096], replicated, may hold values from -0.01171875 to 0.01171875
- lengths: int32 [8], P('dp'), may hold values from 256 to 512, as said below
- offsets: int32 [8], P('dp'), may hold values from 0 to 31
Outputs:
- grad_query: bfloat16 [8, 512, 4096], P('dp', 'seq')
- grad_key: bfloat16 [8, 512, 1024], P('dp', 'seq')
- grad_value: bfloat16 [8, 512, 1024], P('dp', 'seq')
- grad_down: float32 [4096, 64], P('seq')
- grad_up: float32 [64, 4096], P(None, 'seq')
Inputs may be any that keep to these rules, and one draw needn't show every extreme that they name: `lengths`: in every draw at least one rollout has all 512 positions valid.
All inputs are finite; a program needn't handle non-finite values.
Results may differ from a plain program's by a relative error of at most 0.018.
The roundings to bfloat16 on the way count: a program that leaves them out, or rounds other values in their place, can miss the bound.
Values may be sent and summed in bfloat16 or wider, within the bound.
A program may use at most 64 MiB of HBM per device.

v0:
```python
from functools import partial
import jax
import jax.numpy as jnp
from jax import lax
from jax.sharding import PartitionSpec as P

HEAD_WIDTH = 128
rotary_base = 500000.0


def partner_2(value, axis, distance):
    mask = 2**distance
    pairs = [(source, source ^ mask) for source in range(lax.axis_size(axis))]
    return lax.ppermute(value, axis, pairs)


def rotary_tables(length, head_size):
    half_size = head_size // 2
    frequency = rotary_base ** (-(jnp.arange(half_size, dtype=jnp.float32) * 2.0 / head_size))
    angles = jnp.arange(length, dtype=jnp.float32)[:, None] * frequency[None, :]
    return (jnp.cos(angles), jnp.sin(angles))


def rotate(fields, cosine, sine_table, direction):
    half_size = fields.shape[-1] // 2
    first_half = fields[..., :half_size]
    second_half = fields[..., half_size:]
    cos_wide = cosine[:, None, :]
    sin_wide = direction * sine_table[:, None, :]
    return jnp.concatenate(
        [
            first_half * cos_wide - second_half * sin_wide,
            second_half * cos_wide + first_half * sin_wide,
        ],
        axis=-1,
    )


def contract_axes(first_operand, second_operand, first_axis, second_axis):
    return lax.dot_general(
        first_operand,
        second_operand,
        (((first_axis,), (second_axis,)), ((), ())),
        preferred_element_type=jnp.float32,
    )


def block_terms(rot_query, rot_key, value_head, grad_head, offset, begin_row, end_row, score_scale):
    row_index = jnp.arange(begin_row, end_row, dtype=jnp.int32)[:, None]
    col_index = jnp.arange(end_row, dtype=jnp.int32)[None, :]
    visible = (col_index == row_index) | (col_index >= offset) & (col_index <= row_index)
    query_block = rot_query[begin_row:end_row]
    grad_block = grad_head[begin_row:end_row]
    key_block = rot_key[:end_row]
    value_block = value_head[:end_row]
    scores = contract_axes(query_block, key_block, 1, 1) * score_scale
    row_max = jnp.max(jnp.where(visible, scores, -jnp.inf), axis=1, keepdims=True)
    row_total = jnp.sum(jnp.where(visible, jnp.exp(scores - row_max), 0.0), axis=1, keepdims=True)
    grad_prob = contract_axes(grad_block, value_block, 1, 1)
    probability = jnp.where(visible, jnp.exp(scores - row_max), 0.0) / row_total
    row_delta = jnp.sum(probability * grad_prob, axis=1, keepdims=True)
    prob_low = probability.astype(jnp.bfloat16)
    grad_score = (probability * (grad_prob - row_delta) * score_scale).astype(jnp.bfloat16)
    block_grad = jnp.dot(grad_score, key_block, preferred_element_type=jnp.float32)
    key_add = contract_axes(grad_score, query_block, 0, 0)
    value_add = contract_axes(prob_low, grad_block, 0, 0)
    return (block_grad, key_add, value_add)


def head_backward(rot_query, rot_key, value_head, grad_head, offset, block_rows):
    length = rot_query.shape[0]
    head_size = rot_query.shape[1]
    score_scale = head_size ** (-0.5)
    query_parts = []
    key_terms = []
    value_terms = []
    for block_index in range(length // block_rows):
        begin_row = block_index * block_rows
        end_row = begin_row + block_rows
        live_terms = partial(
            block_terms,
            rot_query,
            rot_key,
            value_head,
            grad_head,
            offset,
            begin_row,
            end_row,
            score_scale,
        )
        results = live_terms()
        block_grad, key_add, value_add = results
        query_parts.append(block_grad)
        key_terms.append(jnp.pad(key_add, ((0, length - end_row), (0, 0))))
        value_terms.append(jnp.pad(value_add, ((0, length - end_row), (0, 0))))
    key_accum = key_terms[0]
    value_accum = value_terms[0]
    for term_index in range(1, len(key_terms)):
        key_accum = key_accum + key_terms[term_index]
        value_accum = value_accum + value_terms[term_index]
    return (jnp.concatenate(query_parts, axis=0), key_accum, value_accum)


def arrange_rows(rows, share, part_rows, key_groups):
    rollout_count = rows.shape[0]
    split = rows.reshape(rollout_count, share, part_rows, key_groups, HEAD_WIDTH)
    return jnp.transpose(split, (0, 2, 3, 1, 4)).reshape(
        rollout_count, part_rows, key_groups * share, HEAD_WIDTH
    )


def join_group(paired, share, seq_parts, part_rows):
    my_index = lax.axis_index("seq")
    rollout_count = paired.shape[1]
    local_keys = paired.shape[3]
    joined = paired[None]
    for bit in range(share.bit_length() - 1):
        partner = partner_2(joined, "seq", bit)
        upper = my_index // (1 << bit) % 2
        joined = jnp.where(
            upper == 0,
            jnp.concatenate([joined, partner], axis=0),
            jnp.concatenate([partner, joined], axis=0),
        )
    ordered = joined.reshape(share, 2, rollout_count, seq_parts, part_rows, local_keys, HEAD_WIDTH)
    ordered = jnp.transpose(ordered, (1, 2, 3, 0, 4, 5, 6))
    return ordered.reshape(2, rollout_count, seq_parts * share * part_rows, local_keys, HEAD_WIDTH)


def reduce_group(partial_sums, share, seq_parts, part_rows):
    my_index = lax.axis_index("seq")
    rollout_count = partial_sums.shape[1]
    local_keys = partial_sums.shape[3]
    split = partial_sums.reshape(
        2, rollout_count, seq_parts, share, part_rows, local_keys, HEAD_WIDTH
    )
    split = jnp.transpose(split, (3, 0, 1, 2, 4, 5, 6))
    for bit in reversed(range(share.bit_length() - 1)):
        half = split.shape[0] // 2
        lower_half = split[:half]
        upper_half = split[half:]
        upper = my_index // (1 << bit) % 2
        keep = jnp.where(upper == 0, lower_half, upper_half)
        outgoing = jnp.where(upper == 0, upper_half, lower_half)
        split = keep + partner_2(outgoing.astype(jnp.bfloat16), "seq", bit).astype(outgoing.dtype)
    return split[0].reshape(2, rollout_count, seq_parts * part_rows, local_keys, HEAD_WIDTH)


def on_device(
    queries,
    unrotated_key_rows,
    value_projection_rows,
    attention_output_gradient,
    normed_hidden_input,
    adapter_down_weight,
    adapter_up_weight,
    lengths,
    offsets,
):
    rollout_count = queries.shape[0]
    tokens = queries.shape[1]
    seq_parts = lax.axis_size("seq")
    length = tokens * seq_parts
    query_width = queries.shape[2]
    head_count = query_width // HEAD_WIDTH
    key_groups = unrotated_key_rows.shape[2] // HEAD_WIDTH
    local_heads = head_count // seq_parts
    adapter_rank_size = adapter_down_weight.shape[1]
    share = max(1, seq_parts // key_groups)
    part_rows = tokens // share
    query_tokens = queries.reshape(rollout_count, tokens, head_count, HEAD_WIDTH)
    grad_tokens = attention_output_gradient.reshape(rollout_count, tokens, head_count, HEAD_WIDTH)
    key_arranged = arrange_rows(unrotated_key_rows, share, part_rows, key_groups)
    value_arranged = arrange_rows(value_projection_rows, share, part_rows, key_groups)
    query_heads, key_parted, value_parted, grad_heads = (
        lax.all_to_all(query_tokens, "seq", split_axis=2, concat_axis=1, tiled=True),
        lax.all_to_all(key_arranged, "seq", split_axis=2, concat_axis=1, tiled=True),
        lax.all_to_all(value_arranged, "seq", split_axis=2, concat_axis=1, tiled=True),
        lax.all_to_all(grad_tokens, "seq", split_axis=2, concat_axis=1, tiled=True),
    )
    paired = join_group(jnp.stack([key_parted, value_parted], axis=0), share, seq_parts, part_rows)
    key_heads = paired[0]
    value_heads = paired[1]
    local_keys = key_heads.shape[2]
    cosine, sine_table = rotary_tables(length, HEAD_WIDTH)
    positions = jnp.arange(length, dtype=jnp.int32)
    keep_mask = (positions[None, :] >= offsets[:, None]) & (positions[None, :] < lengths[:, None])
    grad_heads = jnp.where(keep_mask[:, :, None, None], grad_heads, jnp.zeros_like(grad_heads))
    rot_query = rotate(query_heads.astype(jnp.float32), cosine, sine_table, 1.0).astype(
        jnp.bfloat16
    )
    rot_key = rotate(key_heads.astype(jnp.float32), cosine, sine_table, 1.0).astype(jnp.bfloat16)
    block_rows = min(512, length)
    query_rolls = []
    key_rolls = []
    value_rolls = []
    for rollout_slot in range(rollout_count):
        query_list = []
        key_list = []
        value_list = []
        for head_slot in range(local_heads):
            key_slot = head_slot * local_keys // local_heads
            query_grad, key_grad, value_grad = head_backward(
                rot_query[rollout_slot, :, head_slot],
                rot_key[rollout_slot, :, key_slot],
                value_heads[rollout_slot, :, key_slot],
                grad_heads[rollout_slot, :, head_slot],
                offsets[rollout_slot],
                block_rows,
            )
            query_list.append(
                rotate(query_grad[:, None, :], cosine, sine_table, -1.0)[:, 0].astype(jnp.bfloat16)
            )
            key_list.append(
                rotate(key_grad[:, None, :], cosine, sine_table, -1.0)[:, 0].astype(jnp.bfloat16)
            )
            value_list.append(value_grad.astype(jnp.bfloat16))
        query_rolls.append(jnp.stack(query_list, axis=1))
        key_rolls.append(jnp.stack(key_list, axis=1))
        value_rolls.append(jnp.stack(value_list, axis=1))
    query_back = jnp.stack(query_rolls, axis=0)
    key_parts = jnp.stack(key_rolls, axis=0)
    value_parts = jnp.stack(value_rolls, axis=0)
    shared_heads = local_heads // local_keys
    key_local = (
        key_parts.astype(jnp.float32)
        .reshape(rollout_count, length, local_keys, shared_heads, HEAD_WIDTH)
        .sum(axis=3)
    )
    value_local = (
        value_parts.astype(jnp.float32)
        .reshape(rollout_count, length, local_keys, shared_heads, HEAD_WIDTH)
        .sum(axis=3)
    )
    summed = reduce_group(
        jnp.stack([key_local, value_local], axis=0), share, seq_parts, part_rows
    ).astype(jnp.bfloat16)
    query_result, key_result, value_result = (
        lax.all_to_all(query_back, "seq", split_axis=1, concat_axis=2, tiled=True),
        lax.all_to_all(summed[0], "seq", split_axis=1, concat_axis=2, tiled=True),
        lax.all_to_all(summed[1], "seq", split_axis=1, concat_axis=2, tiled=True),
    )
    key_total = jnp.transpose(
        key_result.reshape(rollout_count, part_rows, key_groups, share, HEAD_WIDTH), (0, 3, 1, 2, 4)
    ).reshape(rollout_count, tokens, key_groups * HEAD_WIDTH)
    value_total = jnp.transpose(
        value_result.reshape(rollout_count, part_rows, key_groups, share, HEAD_WIDTH),
        (0, 3, 1, 2, 4),
    ).reshape(rollout_count, tokens, key_groups * HEAD_WIDTH)
    flattened_query = query_result.reshape(rollout_count * tokens, query_width)
    hidden_state = normed_hidden_input.reshape(rollout_count * tokens, normed_hidden_input.shape[2])
    adapter_latent = jnp.dot(
        hidden_state, adapter_down_weight, preferred_element_type=jnp.float32
    ).astype(jnp.bfloat16)
    backward_gradient = contract_axes(flattened_query, adapter_up_weight, 1, 1).astype(jnp.bfloat16)
    joined_terms = lax.psum_scatter(
        jnp.concatenate(
            [
                contract_axes(hidden_state, backward_gradient, 0, 0),
                contract_axes(flattened_query, adapter_latent, 0, 0),
            ],
            axis=1,
        ).astype(jnp.bfloat16),
        "seq",
        scatter_dimension=0,
        tiled=True,
    ).astype(jnp.float32)
    down_local = joined_terms[:, :adapter_rank_size]
    up_local = joined_terms[:, adapter_rank_size:]
    down_sum, up_sum = (
        lax.psum(down_local.astype(jnp.bfloat16), "dp").astype(jnp.float32),
        lax.psum(up_local.astype(jnp.bfloat16), "dp").astype(jnp.float32),
    )
    return (
        flattened_query.reshape(rollout_count, tokens, query_width),
        key_total,
        value_total,
        down_sum,
        up_sum.T,
    )


def solution(mesh):
    in_specs = (
        P("dp", "seq", None),
        P("dp", "seq", None),
        P("dp", "seq", None),
        P("dp", "seq", None),
        P("dp", "seq", None),
        P(),
        P(),
        P("dp"),
        P("dp"),
    )
    out_specs = (
        P("dp", "seq", None),
        P("dp", "seq", None),
        P("dp", "seq", None),
        P("seq", None),
        P(None, "seq"),
    )
    return jax.shard_map(
        on_device, mesh=mesh, in_specs=in_specs, out_specs=out_specs, check_vma=False
    )
```

profile of v0, /device:TPU:0, one launch (start us, length us, event | category | flops | bytes accessed | tf_op | source)
XLA Modules:
  0.0 218.1 jit_solution(3533386464252049813)
XLA Ops:
  7.2 1.9 copy_bitcast_fusion.3
  9.1 5.2 %all-to-all-start.1 = ((bf16[2,64,8,128]{3,1,0,2:T(8,128)(2,1)}), bf16[2,64,8,128]{3,1,0,2:T(8,128)(2,1)S(1)}, u32[]{:S(2)}, u32[]{:S(2)}) async-start(bf16[2,64,8,128]{3,1,0,2:T(8,128)(2,1)} %copy_bitcast_fusion.3), calls=%async_computation.1 | async-start | bytes 524288 | tf_op jit(solution)/shard_map/all_to_all | solution.py:177
  14.3 1.3 fusion.96
  15.6 1.0 fusion.38
  16.6 1.3 copy_bitcast_fusion.1
  17.9 1.3 copy_bitcast_fusion
  19.2 0.8 copy_bitcast_fusion.2
  20.0 1.2 all-to-all-done.1
  21.2 3.4 %all-to-all-start.3 = ((bf16[2,64,8,128]{3,1,0,2:T(8,128)(2,1)}), bf16[2,64,8,128]{3,1,0,2:T(8,128)(2,1)S(1)}, u32[]{:S(2)}, u32[]{:S(2)}) async-start(bf16[2,64,8,128]{3,1,0,2:T(8,128)(2,1)} %copy_bitcast_fusion.2), calls=%async_computation.3 | async-start | bytes 524288 | tf_op jit(solution)/shard_map/all_to_all | solution.py:178
  24.6 0.7 iota_compare_fusion.3
  25.3 6.1 %all-to-all-done.3 = bf16[2,64,8,128]{3,1,0,2:T(8,128)(2,1)S(1)} async-done(((bf16[2,64,8,128]{3,1,0,2:T(8,128)(2,1)}), bf16[2,64,8,128]{3,1,0,2:T(8,128)(2,1)S(1)}, u32[]{:S(2)}, u32[]{:S(2)}) %all-to-all-start.3) | async-done | bytes 262176 | tf_op jit(solution)/shard_map/all_to_all | solution.py:178
  31.4 3.6 %all-to-all-start = ((bf16[2,64,32,128]{3,1,0,2:T(8,128)(2,1)}), bf16[2,64,32,128]{3,1,0,2:T(8,128)(2,1)S(1)}, u32[]{:S(2)}, u32[]{:S(2)}) async-start(bf16[2,64,32,128]{3,1,0,2:T(8,128)(2,1)} %copy_bitcast_fusion.1), calls=%async_computation | async-start | bytes 2097152 | tf_op jit(solution)/shard_map/all_to_all | solution.py:176
  36.2 0.7 fusion.95
  36.9 13.4 %all-to-all-done = bf16[2,64,32,128]{3,1,0,2:T(8,128)(2,1)S(1)} async-done(((bf16[2,64,32,128]{3,1,0,2:T(8,128)(2,1)}), bf16[2,64,32,128]{3,1,0,2:T(8,128)(2,1)S(1)}, u32[]{:S(2)}, u32[]{:S(2)}) %all-to-all-start) | async-done | bytes 1048608 | tf_op jit(solution)/shard_map/all_to_all | solution.py:176
  50.3 4.4 %all-to-all-start.2 = ((bf16[2,64,32,128]{3,1,0,2:T(8,128)(2,1)}), bf16[2,64,32,128]{3,1,0,2:T(8,128)(2,1)}, u32[]{:S(2)}, u32[]{:S(2)}) async-start(bf16[2,64,32,128]{3,1,0,2:T(8,128)(2,1)} %copy_bitcast_fusion), calls=%async_computation.2 | async-start | bytes 2097152 | tf_op jit(solution)/shard_map/all_to_all | solution.py:179
  55.2 0.8 copy-done.25
  56.1 0.8 add_convert_fusion
  56.9 1.3 convolution_multiply_fusion.6
  58.2 1.3 convolution_multiply_fusion.5
  59.6 1.4 convolution_multiply_fusion.4
  61.1 1.3 convolution_multiply_fusion.2
  62.4 1.4 convolution_multiply_fusion.1
  63.8 1.3 convolution_multiply_fusion
  65.1 4.9 %all-to-all-done.2 = bf16[2,64,32,128]{3,1,0,2:T(8,128)(2,1)} async-done(((bf16[2,64,32,128]{3,1,0,2:T(8,128)(2,1)}), bf16[2,64,32,128]{3,1,0,2:T(8,128)(2,1)}, u32[]{:S(2)}, u32[]{:S(2)}) %all-to-all-start.2) | async-done | bytes 1048608 | tf_op jit(solution)/shard_map/all_to_all | solution.py:179
  69.9 1.3 copy.65
  73.1 1.0 fusion.1
  74.8 1.0 fusion.5
  77.5 1.0 fusion.6
  79.2 1.0 fusion.7
  80.2 1.0 fusion.8
  81.8 0.9 multiply_convert_fusion.3
  87.2 0.8 multiply_reduce_fusion.5
  88.0 0.9 multiply_convert_fusion.7
  90.5 0.7 subtract_convert_fusion.17
  91.1 0.7 subtract_convert_fusion.16
  91.9 1.1 pad_maximum_fusion
  93.0 2.4 %copy.68 = bf16[2,512,4,128]{3,2,0,1:T(4,128)(2,1)} copy(bf16[2,512,4,128]{1,3,2,0:T(8,128)(2,1)} %pad_maximum_fusion) | data formatting | bytes 2097152 | tf_op jit(solution)/shard_map/stack | solution.py:221
  95.4 4.2 %all-to-all-start.4 = ((bf16[2,512,4,128]{3,2,0,1:T(4,128)(2,1)}), bf16[2,512,4,128]{3,2,0,1:T(4,128)(2,1)}, u32[]{:S(2)}, u32[]{:S(2)}) async-start(bf16[2,512,4,128]{3,2,0,1:T(4,128)(2,1)} %copy.68), calls=%async_computation.4 | async-start | bytes 2097152 | tf_op jit(solution)/shard_map/all_to_all | solution.py:239
  99.7 1.7 fusion.3
  101.5 1.4 fusion.4
  103.2 1.0 copy.74
  104.2 1.1 convolution_bitcast_fusion.3
  105.3 1.1 convolution_bitcast_fusion.2
  106.3 8.7 %all-to-all-done.4 = bf16[2,512,4,128]{3,2,0,1:T(4,128)(2,1)} async-done(((bf16[2,512,4,128]{3,2,0,1:T(4,128)(2,1)}), bf16[2,512,4,128]{3,2,0,1:T(4,128)(2,1)}, u32[]{:S(2)}, u32[]{:S(2)}) %all-to-all-start.4) | async-done | bytes 1048608 | tf_op jit(solution)/shard_map/all_to_all | solution.py:239
  115.1 3.4 %all-to-all-start.6 = ((bf16[2,512,1,128]{3,0,2,1:T(2,128)(2,1)}), bf16[2,512,1,128]{3,0,2,1:T(2,128)(2,1)S(1)}, u32[]{:S(2)}, u32[]{:S(2)}) async-start(bf16[2,512,1,128]{3,0,2,1:T(2,128)(2,1)} %copy.74), calls=%async_computation.6 | async-start | bytes 524288 | tf_op jit(solution)/shard_map/all_to_all | solution.py:241
  118.5 1.4 copy.69
  119.9 1.8 copy.70
  121.7 2.6 %reshape.691 = bf16[128,4096]{1,0:T(8,128)(2,1)} reshape(bf16[2,64,8,4,128]{4,3,2,1,0:T(4,128)(2,1)} %copy.70) | data formatting | bytes 2097152 | tf_op jit(solution)/shard_map/reshape | solution.py:250
  124.3 3.2 %convolution_convert_fusion = bf16[4096,64]{0,1:T(8,128)(2,1)} fusion(bf16[128,4096]{1,0:T(8,128)(2,1)} %reshape.691, bf16[128,4096]{1,0:T(8,128)(2,1)S(1)} %bitcast.267, bf16[4096,64]{0,1:T(8,128)(2,1)} %param.14), kind=kOutput, calls=%fused_computation | convolution fusion | flops 134488064 | bytes 3145728 | tf_op jit(solution)/shard_map/dot_general | solution.py:40
  127.4 3.1 %fusion = bf16[4096,64]{0,1:T(8,128)(2,1)} fusion(bf16[128,4096]{1,0:T(8,128)(2,1)S(1)} %bitcast.266, bf16[128,4096]{1,0:T(8,128)(2,1)} %reshape.691, bf16[64,4096]{1,0:T(8,128)(2,1)} %param.15), kind=kOutput, calls=%fused_computation.2 | convolution fusion | flops 134488064 | bytes 3145728 | tf_op jit(solution)/shard_map/dot_general | solution.py:40
  130.5 2.3 %pad_maximum_fusion.1 = bf16[4096,128]{0,1:T(8,128)(2,1)} fusion(bf16[4096,64]{0,1:T(8,128)(2,1)} %convolution_convert_fusion, bf16[4096,64]{0,1:T(8,128)(2,1)} %fusion), kind=kLoop, calls=%fused_computation.53 | loop fusion | flops 2097152 | bytes 2097152 | tf_op jit(solution)/shard_map/concatenate | solution.py:257
  132.8 1.5 convolution_bitcast_fusion.1
  138.8 0.7 subtract_convert_fusion.9
  139.5 0.7 subtract_convert_fusion.8
  140.6 0.9 copy.71
  141.5 4.2 %all-to-all-start.5 = ((bf16[2,512,1,128]{3,0,2,1:T(2,128)(2,1)}), bf16[2,512,1,128]{3,0,2,1:T(2,128)(2,1)S(1)}, u32[]{:S(2)}, u32[]{:S(2)}) async-start(bf16[2,512,1,128]{3,0,2,1:T(2,128)(2,1)} %copy.71), calls=%async_computation.5 | async-start | bytes 524288 | tf_op jit(solution)/shard_map/all_to_all | solution.py:240
  145.7 24.8 %reduce-scatter.2.cloned.1.call-done = bf16[512,128]{0,1:T(8,128)(2,1)} async-done(((bf16[4096,128]{0,1:T(8,128)(2,1)}), bf16[512,128]{0,1:T(8,128)(2,1)}) %reduce-scatter.2.cloned.1.call-update) | async-done | bytes 131088 | tf_op jit(solution)/shard_map/reduce_scatter | solution.py:256
  170.5 1.5 slice_bitcast_fusion.24
  172.3 0.8 reshape_transpose_reshape.15
  173.4 0.8 reshape_transpose_reshape.14
  174.2 1.6 reshape_reshape.3
  175.8 32.4 %all-reduce.3.cloned.1.call-done = (bf16[512,64]{0,1:T(8,128)(2,1)}, bf16[64,512]{1,0:T(8,128)(2,1)}) async-done(((bf16[512,64]{0,1:T(8,128)(2,1)}, bf16[64,512]{1,0:T(8,128)(2,1)}), (bf16[512,64]{0,1:T(8,128)(2,1)}, bf16[64,512]{1,0:T(8,128)(2,1)})) %all-reduce.3.cloned.1.call-update) | async-done | bytes 131088 | tf_op jit(solution)/shard_map/psum | solution.py:271
  208.2 1.5 convert_element_type.321
  209.7 1.5 transpose.52
  (149 shorter events, 18.8 us)
Async XLA Ops:
  7.2 117.1 %copy-start = (bf16[2,64,4096]{2,1,0:T(8,128)(2,1)S(1)}, bf16[2,64,4096]{2,1,0:T(8,128)(2,1)}, u32[]{:S(2)}) copy-start(bf16[2,64,4096]{2,1,0:T(8,128)(2,1)} %param.13) | copy-start | bytes 3145732
  7.2 9.4 %copy-start.29 = (bf16[2,64,4096]{2,1,0:T(8,128)(2,1)S(1)}, bf16[2,64,4096]{2,1,0:T(8,128)(2,1)}, u32[]{:S(2)}) copy-start(bf16[2,64,4096]{2,1,0:T(8,128)(2,1)} %param.9) | copy-start | bytes 3145732
  9.1 12.1 %all-to-all-start.1 = ((bf16[2,64,8,128]{3,1,0,2:T(8,128)(2,1)}), bf16[2,64,8,128]{3,1,0,2:T(8,128)(2,1)S(1)}, u32[]{:S(2)}, u32[]{:S(2)}) async-start(bf16[2,64,8,128]{3,1,0,2:T(8,128)(2,1)} %copy_bitcast_fusion.3), calls=%async_computation.1 | async-start | bytes 524288 | tf_op jit(solution)/shard_map/all_to_all | solution.py:177
  14.3 3.7 %copy-start.30 = (bf16[2,64,4096]{2,1,0:T(8,128)(2,1)S(1)}, bf16[2,64,4096]{2,1,0:T(8,128)(2,1)}, u32[]{:S(2)}) copy-start(bf16[2,64,4096]{2,1,0:T(8,128)(2,1)} %param.12) | copy-start | bytes 3145732
  16.6 19.1 %copy-start.24 = (f32[512,64]{1,0:T(8,128)}, f32[512,64]{1,0:T(8,128)S(1)}, u32[]{:S(2)}) copy-start(f32[512,64]{1,0:T(8,128)S(1)} %get-tuple-element.99) | copy-start | bytes 393220
  16.6 19.1 %copy-start.26 = (f32[512,64]{1,0:T(8,128)}, f32[512,64]{1,0:T(8,128)S(1)}, u32[]{:S(2)}) copy-start(f32[512,64]{1,0:T(8,128)S(1)} %get-tuple-element.100) | copy-start | bytes 393220
  16.6 2.6 %copy-start.35 = (bf16[2,64,1024]{2,1,0:T(8,128)(2,1)S(1)}, bf16[2,64,1024]{2,1,0:T(8,128)(2,1)}, u32[]{:S(2)}) copy-start(bf16[2,64,1024]{2,1,0:T(8,128)(2,1)} %param.11) | copy-start | bytes 786436
  17.9 7.3 %copy-start.41 = (s32[2]{0:T(128)S(1)}, s32[2]{0:T(128)}, u32[]{:S(2)}) copy-start(s32[2]{0:T(128)} %param.17) | copy-start | bytes 28
  17.9 7.3 %copy-start.46 = (s32[2]{0:T(128)S(1)}, s32[2]{0:T(128)}, u32[]{:S(2)}) copy-start(s32[2]{0:T(128)} %param.16) | copy-start | bytes 28
  21.2 10.3 %all-to-all-start.3 = ((bf16[2,64,8,128]{3,1,0,2:T(8,128)(2,1)}), bf16[2,64,8,128]{3,1,0,2:T(8,128)(2,1)S(1)}, u32[]{:S(2)}, u32[]{:S(2)}) async-start(bf16[2,64,8,128]{3,1,0,2:T(8,128)(2,1)} %copy_bitcast_fusion.2), calls=%async_computation.3 | async-start | bytes 524288 | tf_op jit(solution)/shard_map/all_to_all | solution.py:178
  31.4 18.9 %all-to-all-start = ((bf16[2,64,32,128]{3,1,0,2:T(8,128)(2,1)}), bf16[2,64,32,128]{3,1,0,2:T(8,128)(2,1)S(1)}, u32[]{:S(2)}, u32[]{:S(2)}) async-start(bf16[2,64,32,128]{3,1,0,2:T(8,128)(2,1)} %copy_bitcast_fusion.1), calls=%async_computation | async-start | bytes 2097152 | tf_op jit(solution)/shard_map/all_to_all | solution.py:176
  50.3 19.6 %all-to-all-start.2 = ((bf16[2,64,32,128]{3,1,0,2:T(8,128)(2,1)}), bf16[2,64,32,128]{3,1,0,2:T(8,128)(2,1)}, u32[]{:S(2)}, u32[]{:S(2)}) async-start(bf16[2,64,32,128]{3,1,0,2:T(8,128)(2,1)} %copy_bitcast_fusion), calls=%async_computation.2 | async-start | bytes 2097152 | tf_op jit(solution)/shard_map/all_to_all | solution.py:179
  55.1 1.0 copy-start.25
  55.1 1.0 copy-start.27
  69.9 1.6 copy-start.34
  71.3 0.9 copy-start.33
  71.5 15.6 %copy-start.28 = (bf16[2,512,4,128]{3,1,2,0:T(8,128)(2,1)}, bf16[2,512,4,128]{3,1,2,0:T(8,128)(2,1)S(1)}, u32[]{:S(2)}) copy-start(bf16[2,512,4,128]{3,1,2,0:T(8,128)(2,1)S(1)} %bitcast_select_fusion) | copy-start | bytes 3145732
  74.8 1.2 copy-start.2
  74.8 1.6 copy-start.22
  74.8 1.9 copy-start.23
  82.7 1.2 copy-start.4
  82.7 1.2 copy-start.7
  82.7 1.2 copy-start.9
  83.3 1.2 copy-start.1
  83.3 1.5 copy-start.19
  83.3 2.0 copy-start.21
  84.0 1.9 copy-start.6
  87.1 0.8 copy-start.42
  87.2 2.3 %copy-start.44 = (f32[512]{0:T(512)}, f32[512]{0:T(512)S(1)}, u32[]{:S(2)}) copy-start(f32[512]{0:T(512)S(1)} %get-tuple-element.10) | copy-start | bytes 6148
  88.9 0.9 copy-start.13
  88.9 1.0 copy-start.15
  88.9 1.3 copy-start.11
  89.9 1.9 copy-start.17
  93.0 6.7 %copy-start.45 = (f32[512]{0:T(512)S(1)}, f32[512]{0:T(512)}, u32[]{:S(2)}) copy-start(f32[512]{0:T(512)} %copy-done.44) | copy-start | bytes 6148
  95.4 19.6 %all-to-all-start.4 = ((bf16[2,512,4,128]{3,2,0,1:T(4,128)(2,1)}), bf16[2,512,4,128]{3,2,0,1:T(4,128)(2,1)}, u32[]{:S(2)}, u32[]{:S(2)}) async-start(bf16[2,512,4,128]{3,2,0,1:T(4,128)(2,1)} %copy.68), calls=%async_computation.4 | async-start | bytes 2097152 | tf_op jit(solution)/shard_map/all_to_all | solution.py:239
  99.7 1.7 copy-start.20
  99.7 1.7 copy-start.43
  101.4 1.4 copy-start.36
  101.4 1.4 copy-start.37
  101.4 1.4 copy-start.38
  101.4 1.4 copy-start.39
  101.4 1.4 copy-start.40
  102.9 1.3 copy-start.10
  103.0 2.2 %copy-start.8 = (bf16[512,512]{0,1:T(8,128)(2,1)S(1)}, bf16[512,512]{0,1:T(8,128)(2,1)}, u32[]{:S(2)}) copy-start(bf16[512,512]{0,1:T(8,128)(2,1)} %copy-done.7) | copy-start | bytes 1572868
  115.1 26.4 %all-to-all-start.6 = ((bf16[2,512,1,128]{3,0,2,1:T(2,128)(2,1)}), bf16[2,512,1,128]{3,0,2,1:T(2,128)(2,1)S(1)}, u32[]{:S(2)}, u32[]{:S(2)}) async-start(bf16[2,512,1,128]{3,0,2,1:T(2,128)(2,1)} %copy.74), calls=%async_computation.6 | async-start | bytes 524288 | tf_op jit(solution)/shard_map/all_to_all | solution.py:241
  118.5 52.1 %reduce-scatter.2.cloned.1.call-start = ((), (), s32[]{:S(2)}) async-start(), calls=%async_computation.8 | async-start | bytes 1179648 | tf_op jit(solution)/shard_map/reduce_scatter | solution.py:256
  132.8 1.5 copy-start.16
  134.3 1.0 copy-start.14
  135.4 1.0 copy-start.12
  136.4 1.0 copy-start.18
  137.4 1.0 copy-start.5
  137.4 1.4 copy-start.32
  137.5 2.0 copy-start.31
  141.4 32.7 %copy-start.3 = (bf16[2,64,8,4,128]{4,3,2,1,0:T(4,128)(2,1)S(1)}, bf16[2,64,8,4,128]{4,3,2,1,0:T(4,128)(2,1)}, u32[]{:S(2)}) copy-start(bf16[2,64,8,4,128]{4,3,2,1,0:T(4,128)(2,1)} %copy.70) | copy-start | bytes 3145732
  141.5 31.7 %all-to-all-start.5 = ((bf16[2,512,1,128]{3,0,2,1:T(2,128)(2,1)}), bf16[2,512,1,128]{3,0,2,1:T(2,128)(2,1)S(1)}, u32[]{:S(2)}, u32[]{:S(2)}) async-start(bf16[2,512,1,128]{3,0,2,1:T(2,128)(2,1)} %copy.71), calls=%async_computation.5 | async-start | bytes 524288 | tf_op jit(solution)/shard_map/all_to_all | solution.py:240
  145.7 62.5 %all-reduce.3.cloned.1.call-start = ((), (), s32[]{:S(2)}) async-start(), calls=%async_computation.9 | async-start | bytes 262144 | tf_op jit(solution)/shard_map/psum | solution.py:271
Sparse Core Ops, SparseCore 0:
  132.9 37.5 reduce-scatter.1
  173.5 34.6 all-reduce.2
where the time goes:
time: 219 us; the launch traced here: 218 us
  waiting for transfers between devices  91.6 us (42%)
  matrix products  35.7 us (16%)
  local copies, waits for them, and re-layouts  30 us (14%)
  starting transfers between devices  28.5 us (13%)
  other arithmetic  17.3 us (8%)
  between operations  14.9 us (7%)
    dot_general x34, matrix products, contract_axes(): lax.dot_general(first_operand, second_operand, (((first_axis,), (second_a...  33.6 us
    psum x1, waiting for transfers between devices, on_device(): lax.psum(down_local.astype(jnp.bfloat16), 'dp').astype(jnp.float32)  32.4 us
    reduce_scatter x1, waiting for transfers between devices, on_device(): lax.psum_scatter(jnp.concatenate([contract_axes(hidden_state, backward_gr...  24.8 us
    all_to_all x1, waiting for transfers between devices, on_device(): lax.all_to_all(query_tokens, 'seq', split_axis=2, concat_axis=1, tiled=True)  13.4 us
    all_to_all x1, waiting for transfers between devices, on_device(): lax.all_to_all(query_back, 'seq', split_axis=1, concat_axis=2, tiled=True)  8.72 us
    all_to_all x1, waiting for transfers between devices, on_device(): lax.all_to_all(value_arranged, 'seq', split_axis=2, concat_axis=1, tiled=...  6.08 us
    unnamed x94, local copies, waits for them, and re-layouts  5.95 us
    all_to_all x1, starting transfers between devices, on_device(): lax.all_to_all(key_arranged, 'seq', split_axis=2, concat_axis=1, tiled=True)  5.2 us
  transfers between devices with their start and end apart: 9, of which 7 were waited for; matrix products, arithmetic and copies ran while one was open for 23% of the time, Pallas kernels for 0%

commit v1 on v0

--- a/solution.py
+++ b/solution.py
@@ -6,6 +6,12 @@
 
 HEAD_WIDTH = 128
 rotary_base = 500000.0
+
+
+def exchange_blocks(value, axis, split, join):
+    pieces = jnp.split(value, lax.axis_size(axis), axis=split)
+    got = lax.all_to_all(jnp.stack(pieces), axis, 0, 0)
+    return jnp.concatenate(got, axis=join)
 
 
 def partner_2(value, axis, distance):
@@ -173,7 +179,7 @@
     key_arranged = arrange_rows(unrotated_key_rows, share, part_rows, key_groups)
     value_arranged = arrange_rows(value_projection_rows, share, part_rows, key_groups)
     query_heads, key_parted, value_parted, grad_heads = (
-        lax.all_to_all(query_tokens, "seq", split_axis=2, concat_axis=1, tiled=True),
+        exchange_blocks(query_tokens, "seq", 2, 1),
         lax.all_to_all(key_arranged, "seq", split_axis=2, concat_axis=1, tiled=True),
         lax.all_to_all(value_arranged, "seq", split_axis=2, concat_axis=1, tiled=True),
         lax.all_to_all(grad_tokens, "seq", split_axis=2, concat_axis=1, tiled=True),

time: 219 us -> 228 us (1.041)
  local copies, waits for them, and re-layouts: 30 us -> 39.4 us
  waiting for transfers between devices: 91.6 us -> 88.4 us
    unnamed x94 -> x98, local copies, waits for them, and re-layouts: 5.95 us -> 14.1 us
  transfers between devices with their start and end apart: 9 -> 9, of which waited for: 7 -> 6; matrix products, arithmetic and copies ran while one was open for 23% -> 26% of each run, Pallas kernels for 0% -> 0%
where the time goes in v1:
time: 228 us; the launch traced here: 227 us
  waiting for transfers between devices  88.4 us (39%)
  local copies, waits for them, and re-layouts  39.4 us (17%)
  matrix products  35.7 us (16%)
  starting transfers between devices  29.3 us (13%)
  other arithmetic  19.2 us (8%)
  between operations  14.9 us (7%)
    dot_general x34, matrix products, contract_axes(): lax.dot_general(first_operand, second_operand, (((first_axis,), (second_a...  33.6 us
    psum x1, waiting for transfers between devices, on_device(): lax.psum(down_local.astype(jnp.bfloat16), 'dp').astype(jnp.float32)  32.4 us
    reduce_scatter x1, waiting for transfers between devices, on_device(): lax.psum_scatter(jnp.concatenate([contract_axes(hidden_state, backward_gr...  24.8 us
    unnamed x98, local copies, waits for them, and re-layouts  14.1 us
    all_to_all x1, waiting for transfers between devices, exchange_blocks(): got = lax.all_to_all(jnp.stack(pieces), axis, 0, 0)  12.5 us
    all_to_all x1, waiting for transfers between devices, on_device(): lax.all_to_all(query_back, 'seq', split_axis=1, concat_axis=2, tiled=True)  8.72 us
    all_to_all x1, waiting for transfers between devices, on_device(): lax.all_to_all(value_arranged, 'seq', split_axis=2, concat_axis=1, tiled=...  6.18 us
    all_to_all x1, starting transfers between devices, on_device(): lax.all_to_all(key_arranged, 'seq', split_axis=2, concat_axis=1, tiled=True)  5.2 us
  transfers between devices with their start and end apart: 9, of which 6 were waited for; matrix products, arithmetic and copies ran while one was open for 26% of the time, Pallas kernels for 0%

profile of v1, /device:TPU:0, one launch (start us, length us, event | category | flops | bytes accessed | tf_op | source)
XLA Modules:
  0.0 227.0 jit_solution(6151959438260258685)
XLA Ops:
  7.2 1.8 copy_bitcast_fusion.2
  9.0 5.2 %all-to-all-start.1 = ((bf16[2,64,8,128]{3,1,0,2:T(8,128)(2,1)}), bf16[2,64,8,128]{3,1,0,2:T(8,128)(2,1)S(1)}, u32[]{:S(2)}, u32[]{:S(2)}) async-start(bf16[2,64,8,128]{3,1,0,2:T(8,128)(2,1)} %copy_bitcast_fusion.2), calls=%async_computation.1 | async-start | bytes 524288 | tf_op jit(solution)/shard_map/all_to_all | solution.py:183
  14.2 1.3 fusion.104
  16.2 0.7 compare_and_fusion
  16.9 1.7 copy_bitcast_fusion.1
  18.6 1.0 fusion.38
  19.6 1.6 copy.84
  22.0 0.7 fusion.56
  23.4 0.7 fusion.54
  24.8 0.7 fusion.52
  25.5 1.3 copy_bitcast_fusion
  27.5 4.2 %all-to-all-start.3 = ((bf16[2,64,8,128]{3,1,0,2:T(8,128)(2,1)}), bf16[2,64,8,128]{3,1,0,2:T(8,128)(2,1)S(1)}, u32[]{:S(2)}, u32[]{:S(2)}) async-start(bf16[2,64,8,128]{3,1,0,2:T(8,128)(2,1)} %copy_bitcast_fusion.1), calls=%async_computation.3 | async-start | bytes 524288 | tf_op jit(solution)/shard_map/all_to_all | solution.py:184
  31.7 0.7 fusion.50
  32.5 6.2 %all-to-all-done.3 = bf16[2,64,8,128]{3,1,0,2:T(8,128)(2,1)S(1)} async-done(((bf16[2,64,8,128]{3,1,0,2:T(8,128)(2,1)}), bf16[2,64,8,128]{3,1,0,2:T(8,128)(2,1)S(1)}, u32[]{:S(2)}, u32[]{:S(2)}) %all-to-all-start.3) | async-done | bytes 262176 | tf_op jit(solution)/shard_map/all_to_all | solution.py:184
  39.3 3.6 %all-to-all-start = ((bf16[8,2,64,4,128]{4,3,2,1,0:T(4,128)(2,1)}), bf16[8,2,64,4,128]{4,3,2,1,0:T(4,128)(2,1)S(1)}, u32[]{:S(2)}, u32[]{:S(2)}) async-start(bf16[8,2,64,4,128]{4,3,2,1,0:T(4,128)(2,1)} %fusion.50), calls=%async_computation | async-start | bytes 2097152 | tf_op jit(solution)/shard_map/all_to_all | solution.py:13
  43.6 1.0 copy.90
  45.7 12.5 %all-to-all-done = bf16[8,2,64,4,128]{4,3,2,1,0:T(4,128)(2,1)S(1)} async-done(((bf16[8,2,64,4,128]{4,3,2,1,0:T(4,128)(2,1)}), bf16[8,2,64,4,128]{4,3,2,1,0:T(4,128)(2,1)S(1)}, u32[]{:S(2)}, u32[]{:S(2)}) %all-to-all-start) | async-done | bytes 1048608 | tf_op jit(solution)/shard_map/all_to_all | solution.py:13
  58.2 1.0 copy-done.24
  59.2 4.4 %all-to-all-start.2 = ((bf16[2,64,32,128]{3,1,0,2:T(8,128)(2,1)}), bf16[2,64,32,128]{3,1,0,2:T(8,128)(2,1)}, u32[]{:S(2)}, u32[]{:S(2)}) async-start(bf16[2,64,32,128]{3,1,0,2:T(8,128)(2,1)} %copy_bitcast_fusion), calls=%async_computation.2 | async-start | bytes 2097152 | tf_op jit(solution)/shard_map/all_to_all | solution.py:185
  63.6 1.4 convert_bitcast_fusion
  66.1 0.8 add_convert_fusion
  66.9 1.3 convolution_multiply_fusion.6
  68.2 1.3 convolution_multiply_fusion.5
  69.6 1.4 convolution_multiply_fusion.4
  71.1 1.3 convolution_multiply_fusion.2
  72.4 1.4 convolution_multiply_fusion.1
  73.8 1.3 convolution_multiply_fusion
  75.1 3.7 %all-to-all-done.2 = bf16[2,64,32,128]{3,1,0,2:T(8,128)(2,1)} async-done(((bf16[2,64,32,128]{3,1,0,2:T(8,128)(2,1)}), bf16[2,64,32,128]{3,1,0,2:T(8,128)(2,1)}, u32[]{:S(2)}, u32[]{:S(2)}) %all-to-all-start.2) | async-done | bytes 1048608 | tf_op jit(solution)/shard_map/all_to_all | solution.py:185
  78.8 1.3 copy.67
  82.0 1.0 fusion.1
  83.7 1.0 fusion.5
  86.4 1.0 fusion.6
  88.1 1.0 fusion.7
  89.1 1.0 fusion.8
  90.7 0.9 multiply_convert_fusion.3
  96.1 0.8 multiply_reduce_fusion.5
  96.9 0.9 multiply_convert_fusion.7
  100.8 1.1 pad_maximum_fusion
  101.9 2.4 %copy.70 = bf16[2,512,4,128]{3,2,0,1:T(4,128)(2,1)} copy(bf16[2,512,4,128]{1,3,2,0:T(8,128)(2,1)} %pad_maximum_fusion) | data formatting | bytes 2097152 | tf_op jit(solution)/shard_map/stack | solution.py:227
  104.3 4.2 %all-to-all-start.4 = ((bf16[2,512,4,128]{3,2,0,1:T(4,128)(2,1)}), bf16[2,512,4,128]{3,2,0,1:T(4,128)(2,1)}, u32[]{:S(2)}, u32[]{:S(2)}) async-start(bf16[2,512,4,128]{3,2,0,1:T(4,128)(2,1)} %copy.70), calls=%async_computation.4 | async-start | bytes 2097152 | tf_op jit(solution)/shard_map/all_to_all | solution.py:245
  108.6 1.7 fusion.3
  110.4 1.4 fusion.4
  112.1 1.0 copy.76
  113.0 1.1 convolution_bitcast_fusion.3
  114.1 1.1 convolution_bitcast_fusion.2
  115.2 8.7 %all-to-all-done.4 = bf16[2,512,4,128]{3,2,0,1:T(4,128)(2,1)} async-done(((bf16[2,512,4,128]{3,2,0,1:T(4,128)(2,1)}), bf16[2,512,4,128]{3,2,0,1:T(4,128)(2,1)}, u32[]{:S(2)}, u32[]{:S(2)}) %all-to-all-start.4) | async-done | bytes 1048608 | tf_op jit(solution)/shard_map/all_to_all | solution.py:245
  123.9 3.4 %all-to-all-start.6 = ((bf16[2,512,1,128]{3,0,2,1:T(2,128)(2,1)}), bf16[2,512,1,128]{3,0,2,1:T(2,128)(2,1)S(1)}, u32[]{:S(2)}, u32[]{:S(2)}) async-start(bf16[2,512,1,128]{3,0,2,1:T(2,128)(2,1)} %copy.76), calls=%async_computation.6 | async-start | bytes 524288 | tf_op jit(solution)/shard_map/all_to_all | solution.py:247
  127.4 1.4 copy.71
  128.8 1.8 copy.72
  130.6 2.6 %reshape.691 = bf16[128,4096]{1,0:T(8,128)(2,1)} reshape(bf16[2,64,8,4,128]{4,3,2,1,0:T(4,128)(2,1)} %copy.72) | data formatting | bytes 2097152 | tf_op jit(solution)/shard_map/reshape | solution.py:256
  133.2 3.2 %convolution_convert_fusion = bf16[4096,64]{0,1:T(8,128)(2,1)} fusion(bf16[128,4096]{1,0:T(8,128)(2,1)} %reshape.691, bf16[128,4096]{1,0:T(8,128)(2,1)S(1)} %bitcast.296, bf16[4096,64]{0,1:T(8,128)(2,1)} %param.14), kind=kOutput, calls=%fused_computation | convolution fusion | flops 134488064 | bytes 3145728 | tf_op jit(solution)/shard_map/dot_general | solution.py:46
  136.3 3.1 %fusion = bf16[4096,64]{0,1:T(8,128)(2,1)} fusion(bf16[128,4096]{1,0:T(8,128)(2,1)S(1)} %bitcast.295, bf16[128,4096]{1,0:T(8,128)(2,1)} %reshape.691, bf16[64,4096]{1,0:T(8,128)(2,1)} %param.15), kind=kOutput, calls=%fused_computation.2 | convolution fusion | flops 134488064 | bytes 3145728 | tf_op jit(solution)/shard_map/dot_general | solution.py:46
  139.4 2.3 pad_maximum_fusion.1
  141.7 1.5 convolution_bitcast_fusion.1
  149.5 0.9 copy.73
  150.4 4.2 %all-to-all-start.5 = ((bf16[2,512,1,128]{3,0,2,1:T(2,128)(2,1)}), bf16[2,512,1,128]{3,0,2,1:T(2,128)(2,1)S(1)}, u32[]{:S(2)}, u32[]{:S(2)}) async-start(bf16[2,512,1,128]{3,0,2,1:T(2,128)(2,1)} %copy.73), calls=%async_computation.5 | async-start | bytes 524288 | tf_op jit(solution)/shard_map/all_to_all | solution.py:246
  154.6 24.8 %reduce-scatter.2.cloned.1.call-done = bf16[512,128]{0,1:T(8,128)(2,1)} async-done(((bf16[4096,128]{0,1:T(8,128)(2,1)}), bf16[512,128]{0,1:T(8,128)(2,1)}) %reduce-scatter.2.cloned.1.call-update) | async-done | bytes 131088 | tf_op jit(solution)/shard_map/reduce_scatter | solution.py:262
  179.4 1.5 slice_bitcast_fusion.32
  181.2 0.8 reshape_transpose_reshape.15
  182.3 0.8 reshape_transpose_reshape.14
  183.1 1.6 reshape_reshape.3
  184.7 32.4 %all-reduce.3.cloned.1.call-done = (bf16[512,64]{0,1:T(8,128)(2,1)}, bf16[64,512]{1,0:T(8,128)(2,1)}) async-done(((bf16[512,64]{0,1:T(8,128)(2,1)}, bf16[64,512]{1,0:T(8,128)(2,1)}), (bf16[512,64]{0,1:T(8,128)(2,1)}, bf16[64,512]{1,0:T(8,128)(2,1)})) %all-reduce.3.cloned.1.call-update) | async-done | bytes 131088 | tf_op jit(solution)/shard_map/psum | solution.py:277
  217.1 1.5 convert_element_type.317
  218.6 1.5 transpose.52
  (152 shorter events, 26.7 us)
Async XLA Ops:
  7.2 126.0 %copy-start = (bf16[2,64,4096]{2,1,0:T(8,128)(2,1)S(1)}, bf16[2,64,4096]{2,1,0:T(8,128)(2,1)}, u32[]{:S(2)}) copy-start(bf16[2,64,4096]{2,1,0:T(8,128)(2,1)} %param.13) | copy-start | bytes 3145732
  9.0 18.5 %all-to-all-start.1 = ((bf16[2,64,8,128]{3,1,0,2:T(8,128)(2,1)}), bf16[2,64,8,128]{3,1,0,2:T(8,128)(2,1)S(1)}, u32[]{:S(2)}, u32[]{:S(2)}) async-start(bf16[2,64,8,128]{3,1,0,2:T(8,128)(2,1)} %copy_bitcast_fusion.2), calls=%async_computation.1 | async-start | bytes 524288 | tf_op jit(solution)/shard_map/all_to_all | solution.py:183
  18.6 6.9 %copy-start.30 = (bf16[2,64,4096]{2,1,0:T(8,128)(2,1)S(1)}, bf16[2,64,4096]{2,1,0:T(8,128)(2,1)}, u32[]{:S(2)}) copy-start(bf16[2,64,4096]{2,1,0:T(8,128)(2,1)} %param.12) | copy-start | bytes 3145732
  19.6 25.0 %copy-start.25 = (f32[512,64]{1,0:T(8,128)}, f32[512,64]{1,0:T(8,128)S(1)}, u32[]{:S(2)}) copy-start(f32[512,64]{1,0:T(8,128)S(1)} %get-tuple-element.99) | copy-start | bytes 393220
  19.6 25.0 %copy-start.27 = (f32[512,64]{1,0:T(8,128)}, f32[512,64]{1,0:T(8,128)S(1)}, u32[]{:S(2)}) copy-start(f32[512,64]{1,0:T(8,128)S(1)} %get-tuple-element.100) | copy-start | bytes 393220
  27.5 11.1 %all-to-all-start.3 = ((bf16[2,64,8,128]{3,1,0,2:T(8,128)(2,1)}), bf16[2,64,8,128]{3,1,0,2:T(8,128)(2,1)S(1)}, u32[]{:S(2)}, u32[]{:S(2)}) async-start(bf16[2,64,8,128]{3,1,0,2:T(8,128)(2,1)} %copy_bitcast_fusion.1), calls=%async_computation.3 | async-start | bytes 524288 | tf_op jit(solution)/shard_map/all_to_all | solution.py:184
  38.6 0.7 copy-start.31
  39.3 18.9 %all-to-all-start = ((bf16[8,2,64,4,128]{4,3,2,1,0:T(4,128)(2,1)}), bf16[8,2,64,4,128]{4,3,2,1,0:T(4,128)(2,1)S(1)}, u32[]{:S(2)}, u32[]{:S(2)}) async-start(bf16[8,2,64,4,128]{4,3,2,1,0:T(4,128)(2,1)} %fusion.50), calls=%async_computation | async-start | bytes 2097152 | tf_op jit(solution)/shard_map/all_to_all | solution.py:13
  58.2 1.0 copy-start.24
  59.2 19.6 %all-to-all-start.2 = ((bf16[2,64,32,128]{3,1,0,2:T(8,128)(2,1)}), bf16[2,64,32,128]{3,1,0,2:T(8,128)(2,1)}, u32[]{:S(2)}, u32[]{:S(2)}) async-start(bf16[2,64,32,128]{3,1,0,2:T(8,128)(2,1)} %copy_bitcast_fusion), calls=%async_computation.2 | async-start | bytes 2097152 | tf_op jit(solution)/shard_map/all_to_all | solution.py:185
  65.0 1.0 copy-start.26
  65.1 1.0 copy-start.28
  78.8 1.6 copy-start.35
  80.2 0.9 copy-start.34
  80.4 15.6 %copy-start.29 = (bf16[2,512,4,128]{3,1,2,0:T(8,128)(2,1)}, bf16[2,512,4,128]{3,1,2,0:T(8,128)(2,1)S(1)}, u32[]{:S(2)}) copy-start(bf16[2,512,4,128]{3,1,2,0:T(8,128)(2,1)S(1)} %bitcast_select_fusion) | copy-start | bytes 3145732
  83.7 1.2 copy-start.2
  83.7 1.6 copy-start.22
  83.7 1.9 copy-start.23
  91.6 1.2 copy-start.4
  91.6 1.2 copy-start.7
  91.6 1.2 copy-start.9
  92.2 1.2 copy-start.1
  92.2 1.5 copy-start.19
  92.2 2.0 copy-start.21
  92.9 1.9 copy-start.6
  96.0 0.8 copy-start.41
  96.0 2.3 %copy-start.43 = (f32[512]{0:T(512)}, f32[512]{0:T(512)S(1)}, u32[]{:S(2)}) copy-start(f32[512]{0:T(512)S(1)} %get-tuple-element.10) | copy-start | bytes 6148
  97.8 0.9 copy-start.13
  97.8 1.0 copy-start.15
  97.8 1.3 copy-start.11
  98.8 1.9 copy-start.17
  101.9 6.7 %copy-start.44 = (f32[512]{0:T(512)S(1)}, f32[512]{0:T(512)}, u32[]{:S(2)}) copy-start(f32[512]{0:T(512)} %copy-done.43) | copy-start | bytes 6148
  104.3 19.6 %all-to-all-start.4 = ((bf16[2,512,4,128]{3,2,0,1:T(4,128)(2,1)}), bf16[2,512,4,128]{3,2,0,1:T(4,128)(2,1)}, u32[]{:S(2)}, u32[]{:S(2)}) async-start(bf16[2,512,4,128]{3,2,0,1:T(4,128)(2,1)} %copy.70), calls=%async_computation.4 | async-start | bytes 2097152 | tf_op jit(solution)/shard_map/all_to_all | solution.py:245
  108.6 1.7 copy-start.20
  108.6 1.7 copy-start.42
  110.3 1.4 copy-start.36
  110.3 1.4 copy-start.37
  110.3 1.4 copy-start.38
  110.3 1.4 copy-start.39
  110.3 1.4 copy-start.40
  111.8 1.3 copy-start.10
  111.9 2.2 copy-start.8
  123.9 26.4 %all-to-all-start.6 = ((bf16[2,512,1,128]{3,0,2,1:T(2,128)(2,1)}), bf16[2,512,1,128]{3,0,2,1:T(2,128)(2,1)S(1)}, u32[]{:S(2)}, u32[]{:S(2)}) async-start(bf16[2,512,1,128]{3,0,2,1:T(2,128)(2,1)} %copy.76), calls=%async_computation.6 | async-start | bytes 524288 | tf_op jit(solution)/shard_map/all_to_all | solution.py:247
  127.4 52.1 %reduce-scatter.2.cloned.1.call-start = ((), (), s32[]{:S(2)}) async-start(), calls=%async_computation.8 | async-start | bytes 1179648 | tf_op jit(solution)/shard_map/reduce_scatter | solution.py:262
  141.7 1.5 copy-start.16
  143.2 1.0 copy-start.14
  144.3 1.0 copy-start.12
  145.3 1.0 copy-start.18
  146.4 1.0 copy-start.5
  146.4 1.4 copy-start.33
  146.4 2.0 copy-start.32
  150.4 32.7 %copy-start.3 = (bf16[2,64,8,4,128]{4,3,2,1,0:T(4,128)(2,1)S(1)}, bf16[2,64,8,4,128]{4,3,2,1,0:T(4,128)(2,1)}, u32[]{:S(2)}) copy-start(bf16[2,64,8,4,128]{4,3,2,1,0:T(4,128)(2,1)} %copy.72) | copy-start | bytes 3145732
  150.4 31.7 %all-to-all-start.5 = ((bf16[2,512,1,128]{3,0,2,1:T(2,128)(2,1)}), bf16[2,512,1,128]{3,0,2,1:T(2,128)(2,1)S(1)}, u32[]{:S(2)}, u32[]{:S(2)}) async-start(bf16[2,512,1,128]{3,0,2,1:T(2,128)(2,1)} %copy.73), calls=%async_computation.5 | async-start | bytes 524288 | tf_op jit(solution)/shard_map/all_to_all | solution.py:246
  154.6 62.5 %all-reduce.3.cloned.1.call-start = ((), (), s32[]{:S(2)}) async-start(), calls=%async_computation.9 | async-start | bytes 262144 | tf_op jit(solution)/shard_map/psum | solution.py:277
Sparse Core Ops, SparseCore 0:
  141.8 37.5 reduce-scatter.1
  182.4 34.6 all-reduce.2
